TPU v7x, 32 devices: a whole 2x2x4 slice. The times are simulated.
32 devices in a mesh: dp: 8 (over z, y), tensor: 4 (over x, core).
Axes of the slice: x: 2, y: 2, z: 4, core: 2. Of those that a mesh axis runs over, the one named last changes fastest.
Arguments:
- tokens: bfloat16 [1024, 16, 768], P(('dp', 'tensor')), may hold values from -6 to 6
- lengths: int32 [16], replicated, may hold values from 1 to 1024, 12288 in all
- dealing: int32 [16], replicated, may hold values from 0 to 15, each once
- project_weight: bfloat16 [768, 2304], P('dp', 'tensor'), may hold values from -0.21875 to 0.21875
- query_projection_bias: float32 [768], replicated, may hold values from -3 to 3
- value_projection_bias: float32 [768], replicated, may hold values from -3 to 3
- attention_output_weight: bfloat16 [768, 768], P('dp', 'tensor'), may hold values from -3.5 to 3.5
- attention_output_bias: float32 [768], replicated, may hold values from -3 to 3
- first_gain: float32 [768], replicated, may hold values from 0.5 to 1.5
- first_shift: float32 [768], replicated, may hold values from -3 to 3
- feed_input_weight: bfloat16 [768, 3072], P('dp', 'tensor'), may hold values from -0.21875 to 0.21875
- feed_input_bias: float32 [3072], replicated, may hold values from -3 to 3
- feed_output_weight: bfloat16 [768, 3072], P('dp', 'tensor'), may hold values from -0.109375 to 0.109375
- feed_output_bias: float32 [768], replicated, may hold values from -3 to 3
- second_gain: float32 [768], replicated, may hold values from 0.5 to 1.5
- second_shift: float32 [768], replicated, may hold values from -3 to 3
- output_grad: bfloat16 [1024, 16, 768], P(('dp', 'tensor')), may hold values from -6 to 6
Outputs:
- layer_output: bfloat16 [1024, 16, 768], P('tensor', 'dp')
- tokens_grad: bfloat16 [1024, 16, 768], P(('dp', 'tensor'))
- project_grad: float32 [768, 2304], P('dp', 'tensor')
- query_bias_grad: float32 [768], P(('dp', 'tensor'))
- value_bias_grad: float32 [768], P(('dp', 'tensor'))
- output_weight_grad: float32 [768, 768], P('dp', 'tensor')
- output_bias_grad: float32 [768], P(('dp', 'tensor'))
- first_gain_grad: float32 [768], P(('dp', 'tensor'))
- first_shift_grad: float32 [768], P(('dp', 'tensor'))
- up_weight_grad: float32 [768, 3072], P('dp', 'tensor')
- up_bias_grad: float32 [3072], P(('dp', 'tensor'))
- down_weight_grad: float32 [768, 3072], P('dp', 'tensor')
- down_bias_grad: float32 [768], P(('dp', 'tensor'))
- second_gain_grad: float32 [768], P(('dp', 'tensor'))
- second_shift_grad: float32 [768], P(('dp', 'tensor'))
Inputs may be any that keep to these rules, and one draw needn't show every extreme that they name: `lengths`: the longest sequence has exactly 1024 tokens. A permutation: sequence s is processed in slot dealing[s], and slot q belongs to data index q // 2.
All inputs are finite; a program needn't handle non-finite values.
Results may differ from a plain program's by a relative error of at most 0.022.
Values may be sent and summed in bfloat16 or wider, within the bound.
A program may use at most 128 MiB of HBM per device.

v0:
```python
from functools import partial
import jax
import jax.numpy as jnp
from jax import lax
from jax.sharding import PartitionSpec as P

HD = 64
EPSILON = 1e-12
MASKED = -1e30


def norm_forward(value, gain, shift):
    centred = value - jnp.mean(value, axis=-1, keepdims=True)
    inverse = lax.rsqrt(jnp.mean(centred * centred, axis=-1, keepdims=True) + EPSILON)
    normed = centred * inverse
    return (normed * gain + shift, normed, inverse)


def norm_backward(upstream, normed, inverse, gain):
    scaled = upstream * gain
    first_mean = jnp.mean(scaled, axis=-1, keepdims=True)
    second_mean = jnp.mean(scaled * normed, axis=-1, keepdims=True)
    return inverse * (scaled - first_mean - normed * second_mean)


def spread_block(values, block_index, length_total):
    blank = jnp.zeros((length_total,), jnp.float32)
    return lax.dynamic_update_slice_in_dim(blank, values, block_index * values.shape[0], 0)


def gather_rows(block):
    return lax.all_gather(block, "tensor", axis=0, tiled=True)


def scatter_rows(partial_sum):
    return lax.psum_scatter(
        partial_sum.astype(jnp.bfloat16), "tensor", scatter_dimension=0, tiled=True
    ).astype(jnp.float32)


def scatter_weight(grad):
    return lax.psum_scatter(
        grad.astype(jnp.bfloat16), "dp", scatter_dimension=0, tiled=True
    ).astype(jnp.float32)


def on_device(
    tokens,
    lengths,
    dealing,
    project_weight,
    query_projection_bias,
    value_projection_bias,
    attention_output_weight,
    attention_output_bias,
    first_gain,
    first_shift,
    feed_input_weight,
    feed_input_bias,
    feed_output_weight,
    feed_output_bias,
    second_gain,
    second_shift,
    output_grad,
):
    n_data = lax.axis_size("dp")
    n_tensor = lax.axis_size("tensor")
    n_all = n_data * n_tensor
    data_index = lax.axis_index("dp")
    tensor_index = lax.axis_index("tensor")
    seq_total = dealing.shape[0]
    seq_here = seq_total // n_data
    piece_rows = tokens.shape[0]
    local_rows = piece_rows * n_data
    seq_rows = local_rows * n_tensor
    width = tokens.shape[2]
    head_cols = attention_output_weight.shape[1]
    heads_here = head_cols // HD
    hidden_cols = feed_input_weight.shape[1]
    score_scale = HD ** (-0.5)
    slot_ids = jnp.arange(seq_total, dtype=jnp.int32)
    placing = (dealing[None, :] == slot_ids[:, None]).astype(jnp.bfloat16)
    send_tokens = jnp.einsum(
        "qs,psd->pqd", placing, tokens, preferred_element_type=jnp.float32
    ).astype(jnp.bfloat16)
    send_grad = jnp.einsum(
        "qs,psd->pqd", placing, output_grad, preferred_element_type=jnp.float32
    ).astype(jnp.bfloat16)
    tokens_here = lax.all_to_all(send_tokens, "dp", split_axis=1, concat_axis=0, tiled=True)
    cotangent_here = lax.all_to_all(send_grad, "dp", split_axis=1, concat_axis=0, tiled=True)
    my_slots = data_index * seq_here + jnp.arange(seq_here, dtype=jnp.int32)
    mine = dealing[None, :] == my_slots[:, None]
    seq_length = jnp.sum(jnp.where(mine, lengths[None, :], 0), axis=1)
    row_ids = jnp.arange(seq_rows, dtype=jnp.int32)
    owner_rows = row_ids // local_rows
    inner_rows = row_ids % local_rows
    position = (
        inner_rows // piece_rows * n_tensor + owner_rows
    ) * piece_rows + inner_rows % piece_rows
    key_valid = position[None, :] < seq_length[:, None]
    project_full = lax.all_gather(project_weight, "dp", axis=0, tiled=True)
    output_full = lax.all_gather(attention_output_weight, "dp", axis=0, tiled=True)
    up_full = lax.all_gather(feed_input_weight, "dp", axis=0, tiled=True)
    down_full = lax.all_gather(feed_output_weight, "dp", axis=0, tiled=True)
    query_part = lax.dynamic_slice_in_dim(
        query_projection_bias, tensor_index * head_cols, head_cols
    )
    value_part = lax.dynamic_slice_in_dim(
        value_projection_bias, tensor_index * head_cols, head_cols
    )
    project_bias = jnp.concatenate([query_part, jnp.zeros_like(query_part), value_part])
    up_bias_here = lax.dynamic_slice_in_dim(
        feed_input_bias, tensor_index * hidden_cols, hidden_cols
    )

    def split_heads(qkv_block):
        query_rows = qkv_block[:, :head_cols].reshape(seq_rows, heads_here, HD)
        key_rows = qkv_block[:, head_cols : 2 * head_cols].reshape(seq_rows, heads_here, HD)
        value_rows = qkv_block[:, 2 * head_cols :].reshape(seq_rows, heads_here, HD)
        return (query_rows, key_rows, value_rows)

    def masked_scores(query_rows, key_rows, valid_keys):
        raw_scores = (
            jnp.einsum("qhe,khe->hqk", query_rows, key_rows, preferred_element_type=jnp.float32)
            * score_scale
        )
        return jnp.where(valid_keys[None, None, :], raw_scores, MASKED)

    def attend(qkv_block, valid_keys):
        query_rows, key_rows, value_rows = split_heads(qkv_block)
        scores = masked_scores(query_rows, key_rows, valid_keys)
        row_max = jnp.max(scores, axis=-1, keepdims=True)
        exponent = jnp.exp(scores - row_max)
        row_total = jnp.sum(exponent, axis=-1, keepdims=True)
        weights = (exponent / row_total).astype(jnp.bfloat16)
        mixed_heads = jnp.einsum(
            "hqk,khe->qhe", weights, value_rows, preferred_element_type=jnp.float32
        )
        return (
            mixed_heads.reshape(seq_rows, head_cols).astype(jnp.bfloat16),
            (row_max + jnp.log(row_total))[..., 0],
        )

    def attend_back(qkv_block, valid_keys, row_lse, grad_block):
        query_rows, key_rows, value_rows = split_heads(qkv_block)
        weights = jnp.exp(masked_scores(query_rows, key_rows, valid_keys) - row_lse[..., None])
        grad_heads = grad_block.reshape(seq_rows, heads_here, HD)
        grad_weights = jnp.einsum(
            "qhe,khe->hqk", grad_heads, value_rows, preferred_element_type=jnp.float32
        )
        inner_sum = jnp.sum(weights * grad_weights, axis=-1, keepdims=True)
        grad_scores = (weights * (grad_weights - inner_sum)).astype(jnp.bfloat16)
        grad_query = (
            jnp.einsum("hqk,khe->qhe", grad_scores, key_rows, preferred_element_type=jnp.float32)
            * score_scale
        )
        grad_key = (
            jnp.einsum("hqk,qhe->khe", grad_scores, query_rows, preferred_element_type=jnp.float32)
            * score_scale
        )
        grad_value = jnp.einsum(
            "hqk,qhe->khe",
            weights.astype(jnp.bfloat16),
            grad_heads,
            preferred_element_type=jnp.float32,
        )
        joined = jnp.concatenate(
            [
                grad_query.reshape(seq_rows, head_cols),
                grad_key.reshape(seq_rows, head_cols),
                grad_value.reshape(seq_rows, head_cols),
            ],
            axis=-1,
        )
        return joined.astype(jnp.bfloat16)

    gelu_exact = partial(jax.nn.gelu, approximate=False)
    seqs = range(seq_here)
    inputs_full = [gather_rows(tokens_here[:, s, :]) for s in seqs]
    projected = [
        (
            jnp.dot(inputs_full[s], project_full, preferred_element_type=jnp.float32) + project_bias
        ).astype(jnp.bfloat16)
        for s in seqs
    ]
    attended = [attend(projected[s], key_valid[s]) for s in seqs]
    mixed = [a[0] for a in attended]
    log_total = [a[1] for a in attended]
    branch = [
        scatter_rows(
            lax.dot_general(
                mixed[s], output_full, (((1,), (1,)), ((), ())), preferred_element_type=jnp.float32
            )
        )
        for s in seqs
    ]
    first = [
        norm_forward(
            tokens_here[:, s, :].astype(jnp.float32) + branch[s] + attention_output_bias,
            first_gain,
            first_shift,
        )
        for s in seqs
    ]
    first_full = [gather_rows(first[s][0].astype(jnp.bfloat16)) for s in seqs]
    preact = [
        jnp.dot(first_full[s], up_full, preferred_element_type=jnp.float32) + up_bias_here
        for s in seqs
    ]
    gelu_pairs = [jax.vjp(gelu_exact, preact[s]) for s in seqs]
    hidden = [g[0].astype(jnp.bfloat16) for g in gelu_pairs]
    feed = [
        scatter_rows(
            lax.dot_general(
                hidden[s], down_full, (((1,), (1,)), ((), ())), preferred_element_type=jnp.float32
            )
        )
        for s in seqs
    ]
    second = [
        norm_forward(first[s][0] + feed[s] + feed_output_bias, second_gain, second_shift)
        for s in seqs
    ]
    layer_output = jnp.stack([second[s][0] for s in seqs], axis=1).astype(jnp.bfloat16)
    cot = [cotangent_here[:, s, :].astype(jnp.float32) for s in seqs]
    second_gain_part = sum((jnp.sum(cot[s] * second[s][1], axis=0) for s in seqs))
    second_shift_part = sum((jnp.sum(cot[s], axis=0) for s in seqs))
    grad_second = [norm_backward(cot[s], second[s][1], second[s][2], second_gain) for s in seqs]
    down_bias_part = sum((jnp.sum(grad_second[s], axis=0) for s in seqs))
    grad_feed_full = [gather_rows(grad_second[s].astype(jnp.bfloat16)) for s in seqs]
    grad_hidden = [
        jnp.dot(grad_feed_full[s], down_full, preferred_element_type=jnp.float32) for s in seqs
    ]
    down_grad = sum(
        (
            lax.dot_general(
                grad_feed_full[s],
                hidden[s],
                (((0,), (0,)), ((), ())),
                preferred_element_type=jnp.float32,
            )
            for s in seqs
        )
    )
    down_shard = scatter_weight(down_grad)
    grad_preact = [gelu_pairs[s][1](grad_hidden[s])[0].astype(jnp.bfloat16) for s in seqs]
    up_grad = sum(
        (
            lax.dot_general(
                first_full[s],
                grad_preact[s],
                (((0,), (0,)), ((), ())),
                preferred_element_type=jnp.float32,
            )
            for s in seqs
        )
    )
    up_shard = scatter_weight(up_grad)
    up_bias_part = sum((jnp.sum(grad_preact[s], axis=0, dtype=jnp.float32) for s in seqs))
    grad_first = [
        grad_second[s]
        + scatter_rows(
            lax.dot_general(
                grad_preact[s],
                up_full,
                (((1,), (1,)), ((), ())),
                preferred_element_type=jnp.float32,
            )
        )
        for s in seqs
    ]
    first_gain_part = sum((jnp.sum(grad_first[s] * first[s][1], axis=0) for s in seqs))
    first_shift_part = sum((jnp.sum(grad_first[s], axis=0) for s in seqs))
    grad_residual = [
        norm_backward(grad_first[s], first[s][1], first[s][2], first_gain) for s in seqs
    ]
    output_bias_part = sum((jnp.sum(grad_residual[s], axis=0) for s in seqs))
    early_vectors = jnp.concatenate(
        [
            v.reshape(n_all, -1)
            for v in (
                output_bias_part,
                first_gain_part,
                first_shift_part,
                spread_block(up_bias_part, tensor_index, hidden_cols * n_tensor),
                down_bias_part,
                second_gain_part,
                second_shift_part,
            )
        ],
        axis=1,
    )
    early_reduced = lax.psum_scatter(
        early_vectors, ("dp", "tensor"), scatter_dimension=0, tiled=True
    )[0]
    branch_grad_full = [gather_rows(grad_residual[s].astype(jnp.bfloat16)) for s in seqs]
    grad_mixed = [
        jnp.dot(branch_grad_full[s], output_full, preferred_element_type=jnp.float32).astype(
            jnp.bfloat16
        )
        for s in seqs
    ]
    output_grad_weight = sum(
        (
            lax.dot_general(
                branch_grad_full[s],
                mixed[s],
                (((0,), (0,)), ((), ())),
                preferred_element_type=jnp.float32,
            )
            for s in seqs
        )
    )
    output_shard = scatter_weight(output_grad_weight)
    grad_projected = [
        attend_back(projected[s], key_valid[s], log_total[s], grad_mixed[s]) for s in seqs
    ]
    project_grad = sum(
        (
            lax.dot_general(
                inputs_full[s],
                grad_projected[s],
                (((0,), (0,)), ((), ())),
                preferred_element_type=jnp.float32,
            )
            for s in seqs
        )
    )
    project_shard = scatter_weight(project_grad)
    bias_sums = sum((jnp.sum(grad_projected[s], axis=0, dtype=jnp.float32) for s in seqs))
    late_vectors = jnp.concatenate(
        [
            spread_block(bias_sums[:head_cols], tensor_index, width).reshape(n_all, -1),
            spread_block(bias_sums[2 * head_cols :], tensor_index, width).reshape(n_all, -1),
        ],
        axis=1,
    )
    late_reduced = lax.psum_scatter(
        late_vectors, ("dp", "tensor"), scatter_dimension=0, tiled=True
    )[0]
    grad_inputs = [
        grad_residual[s]
        + scatter_rows(
            lax.dot_general(
                grad_projected[s],
                project_full,
                (((1,), (1,)), ((), ())),
                preferred_element_type=jnp.float32,
            )
        )
        for s in seqs
    ]
    grad_here = jnp.stack(grad_inputs, axis=1).astype(jnp.bfloat16)
    returned = lax.all_to_all(grad_here, "dp", split_axis=0, concat_axis=1, tiled=True)
    tokens_grad = jnp.einsum(
        "qs,pqd->psd", placing, returned, preferred_element_type=jnp.float32
    ).astype(jnp.bfloat16)
    vec_block = width // n_all
    early_split = [vec_block] * 3 + [hidden_cols * n_tensor // n_all] + [vec_block] * 3
    offsets = [sum(early_split[:k]) for k in range(len(early_split) + 1)]
    early = [early_reduced[offsets[k] : offsets[k + 1]] for k in range(len(early_split))]
    late = [late_reduced[:vec_block], late_reduced[vec_block:]]
    return (
        layer_output,
        tokens_grad,
        project_shard,
        late[0],
        late[1],
        output_shard,
        early[0],
        early[1],
        early[2],
        up_shard,
        early[3],
        down_shard,
        early[4],
        early[5],
        early[6],
    )


def solution(mesh):
    in_specs = (
        P(("dp", "tensor"), None, None),
        P(),
        P(),
        P("dp", "tensor"),
        P(),
        P(),
        P("dp", "tensor"),
        P(),
        P(),
        P(),
        P("dp", "tensor"),
        P(),
        P("dp", "tensor"),
        P(),
        P(),
        P(),
        P(("dp", "tensor"), None, None),
    )
    out_specs = (
        P("tensor", "dp", None),
        P(("dp", "tensor"), None, None),
        P("dp", "tensor"),
        P(("dp", "tensor")),
        P(("dp", "tensor")),
        P("dp", "tensor"),
        P(("dp", "tensor")),
        P(("dp", "tensor")),
        P(("dp", "tensor")),
        P("dp", "tensor"),
        P(("dp", "tensor")),
        P("dp", "tensor"),
        P(("dp", "tensor")),
        P(("dp", "tensor")),
        P(("dp", "tensor")),
    )
    return jax.shard_map(
        on_device, mesh=mesh, in_specs=in_specs, out_specs=out_specs, check_vma=False
    )
```

profile of v0, /device:TPU:0, one launch (start us, length us, event | category | flops | bytes accessed | tf_op | source)
XLA Modules:
  0.0 850.2 jit_solution(14724456239618128440)
XLA Ops:
  10.6 27.4 %all_to_all.54 = bf16[32,16,768]{2,0,1:T(8,128)(2,1)S(1)} all-to-all(bf16[32,16,768]{2,0,1:T(8,128)(2,1)S(1)} %copy.78), channel_id=1, replica_groups=mesh['dp'=8,'tensor'=4] {'dp'}, dimensions={1} | all-to-all | bytes 1572864 | tf_op jit(solution)/shard_map/all_to_all | solution.py:89
  41.7 31.2 %all_gather.38 = bf16[768,192]{1,0:T(8,128)(2,1)S(1)} all-gather(bf16[96,192]{1,0:T(8,128)(2,1)S(1)} %copy-done.49), channel_id=1, replica_groups=mesh['dp'=8,'tensor'=4] {'dp'}, dimensions={0}, use_global_device_ids=true | all-gather | bytes 331776 | tf_op jit(solution)/shard_map/all_gather | solution.py:102
  72.9 32.5 %all_gather.37 = bf16[768,576]{1,0:T(8,128)(2,1)S(1)} all-gather(bf16[96,576]{1,0:T(8,128)(2,1)S(1)} %copy-done.45), channel_id=1, replica_groups=mesh['dp'=8,'tensor'=4] {'dp'}, dimensions={0}, use_global_device_ids=true | all-gather | bytes 995328 | tf_op jit(solution)/shard_map/all_gather | solution.py:101
  136.4 14.9 %reduce-scatter.13.cloned.1.call-done = bf16[256,768]{1,0:T(8,128)(2,1)} async-done(((bf16[1024,768]{1,0:T(8,128)(2,1)}), bf16[256,768]{1,0:T(8,128)(2,1)}) %reduce-scatter.13.cloned.1.call-update) | async-done | bytes 393232 | tf_op jit(solution)/shard_map/reduce_scatter | solution.py:36
  152.6 29.1 %reduce-scatter.17.cloned.1.call-done = bf16[256,768]{1,0:T(8,128)(2,1)} async-done(((bf16[1024,768]{1,0:T(8,128)(2,1)}), bf16[256,768]{1,0:T(8,128)(2,1)}) %reduce-scatter.17.cloned.1.call-update) | async-done | bytes 393232 | tf_op jit(solution)/shard_map/reduce_scatter | solution.py:36
  189.2 17.3 %all-gather.19.cloned.1.call-done = bf16[1024,768]{1,0:T(8,128)(2,1)} async-done(((bf16[256,768]{1,0:T(8,128)(2,1)}), bf16[1024,768]{1,0:T(8,128)(2,1)}) %all-gather.19.cloned.1.call-update) | async-done | bytes 1572880 | tf_op jit(solution)/shard_map/all_gather | solution.py:32
  206.5 4.9 fusion.119
  211.4 16.7 %all-gather.13.cloned.1.call-done = bf16[1024,768]{1,0:T(8,128)(2,1)} async-done(((bf16[256,768]{1,0:T(8,128)(2,1)}), bf16[1024,768]{1,0:T(8,128)(2,1)}) %all-gather.13.cloned.1.call-update) | async-done | bytes 1572880 | tf_op jit(solution)/shard_map/all_gather | solution.py:32
  228.1 17.3 %multiply_convert_fusion.3 = (bf16[1024,768]{1,0:T(8,128)(2,1)}, f32[1024,768]{1,0:T(8,128)}, bf16[1024,768]{1,0:T(8,128)(2,1)}, f32[1024,768]{1,0:T(8,128)}, f32[1024,768]{1,0:T(8,128)}) fusion(f32[768]{0:T(1024)S(1)} %dynamic_slice.11, f32[1024,768]{1,0:T(8,128)} %fusion.119, bf16[1024,768]{1,0:T(8,128)(2,1)} %all-gather.13.cloned.1.call-done, ...), kind=kOutput, calls=%fused_computation.43 | convolution fusion | flops 1311768576 | bytes 18484224 | tf_op jit(solution)/shard_map/dot_general | solution.py:207
  245.4 26.3 %all-gather.17.cloned.1.call-done = bf16[768,768]{1,0:T(8,128)(2,1)} async-done(((bf16[96,768]{1,0:T(8,128)(2,1)}), bf16[768,768]{1,0:T(8,128)(2,1)}) %all-gather.17.cloned.1.call-update) | async-done | bytes 1179664 | tf_op jit(solution)/shard_map/all_gather | solution.py:104
  276.1 4.4 convolution_convert_fusion.4
  282.0 21.2 %all_to_all.55 = bf16[32,16,768]{2,0,1:T(8,128)(2,1)S(1)} all-to-all(bf16[32,16,768]{2,0,1:T(8,128)(2,1)S(1)} %copy.83), channel_id=1, replica_groups=mesh['dp'=8,'tensor'=4] {'dp'}, dimensions={1} | all-to-all | bytes 1572864 | tf_op jit(solution)/shard_map/all_to_all | solution.py:90
  303.4 29.6 %reduce-scatter.19.cloned.1.call-done = bf16[256,768]{1,0:T(8,128)(2,1)} async-done(((bf16[1024,768]{1,0:T(8,128)(2,1)}), bf16[256,768]{1,0:T(8,128)(2,1)}) %reduce-scatter.19.cloned.1.call-update) | async-done | bytes 393232 | tf_op jit(solution)/shard_map/reduce_scatter | solution.py:36
  341.0 18.6 %all-gather.21.cloned.1.call-done = bf16[1024,768]{1,0:T(8,128)(2,1)} async-done(((bf16[256,768]{1,0:T(8,128)(2,1)}), bf16[1024,768]{1,0:T(8,128)(2,1)}) %all-gather.21.cloned.1.call-update) | async-done | bytes 1572880 | tf_op jit(solution)/shard_map/all_gather | solution.py:32
  359.7 4.8 fusion.120
  364.4 16.3 %all-gather.25.cloned.1.call-done = bf16[1024,768]{1,0:T(8,128)(2,1)} async-done(((bf16[256,768]{1,0:T(8,128)(2,1)}), bf16[1024,768]{1,0:T(8,128)(2,1)}) %all-gather.25.cloned.1.call-update) | async-done | bytes 1572880 | tf_op jit(solution)/shard_map/all_gather | solution.py:32
  380.8 11.5 %convert_reduce_fusion = (f32[768]{0:T(1024)}, bf16[1024,768]{1,0:T(8,128)(2,1)}, f32[768]{0:T(1024)}, bf16[1024,768]{1,0:T(8,128)(2,1)S(1)}) fusion(f32[1024,768]{1,0:T(8,128)} %get-tuple-element.152, f32[1024,768]{1,0:T(8,128)} %fusion.119, f32[768]{0:T(1024)} %copy-done.58, f32[1024,768]{1,0:T(8,128)} %fusion.120, f32[1024,768]{1,0:T(8,128)} %get-tuple-element.119, ...), kind=kOutput, calls=%fused_computation.26 | convolution fusion | flops 1234696704 | bytes 21636096 | tf_op jit(solution)/shard_map/dot_general | solution.py:232
  400.6 23.6 %reduce-scatter.21.cloned.1.call-done = bf16[256,768]{1,0:T(8,128)(2,1)} async-done(((bf16[1024,768]{1,0:T(8,128)(2,1)}), bf16[256,768]{1,0:T(8,128)(2,1)}) %reduce-scatter.21.cloned.1.call-update) | async-done | bytes 393232 | tf_op jit(solution)/shard_map/reduce_scatter | solution.py:36
  424.1 30.4 %reduce-scatter.25.cloned.1.call-done = bf16[256,768]{1,0:T(8,128)(2,1)} async-done(((bf16[1024,768]{1,0:T(8,128)(2,1)}), bf16[256,768]{1,0:T(8,128)(2,1)}) %reduce-scatter.25.cloned.1.call-update) | async-done | bytes 393232 | tf_op jit(solution)/shard_map/reduce_scatter | solution.py:36
  466.3 15.8 %all-gather.27.cloned.1.call-done = bf16[1024,768]{1,0:T(8,128)(2,1)} async-done(((bf16[256,768]{1,0:T(8,128)(2,1)}), bf16[1024,768]{1,0:T(8,128)(2,1)}) %all-gather.27.cloned.1.call-update) | async-done | bytes 1572880 | tf_op jit(solution)/shard_map/all_gather | solution.py:32
  484.3 6.1 multiply_reduce_fusion
  493.0 5.2 multiply_convert_fusion
  498.3 5.0 fusion.38
  511.7 6.4 multiply_reduce_fusion.1
  520.7 5.2 multiply_convert_fusion.1
  525.9 5.0 fusion.36
  571.8 5.5 all-to-all-start.2
  578.2 62.9 %reduce-scatter.35.cloned.1.call-done = bf16[96,768]{1,0:T(8,128)(2,1)} async-done(((bf16[768,768]{1,0:T(8,128)(2,1)}), bf16[96,768]{1,0:T(8,128)(2,1)}) %reduce-scatter.35.cloned.1.call-update) | async-done | bytes 147472 | tf_op jit(solution)/shard_map/reduce_scatter | solution.py:42
  642.7 65.5 %reduce-scatter.33.cloned.1.call-done = bf16[96,768]{1,0:T(8,128)(2,1)} async-done(((bf16[768,768]{1,0:T(8,128)(2,1)}), bf16[96,768]{1,0:T(8,128)(2,1)}) %reduce-scatter.33.cloned.1.call-update) | async-done | bytes 147472 | tf_op jit(solution)/shard_map/reduce_scatter | solution.py:42
  716.4 40.2 %all-reduce.2 = (f32[32,48]{1,0:T(8,128)S(1)}, f32[32,240]{1,0:T(8,128)S(1)}) all-reduce(f32[32,48]{1,0:T(8,128)S(1)} %pad_maximum_fusion.4, f32[32,240]{1,0:T(8,128)} %concatenate.21), channel_id=13, replica_groups=mesh['dp'=8,'tensor'=4] {'dp','tensor'}, use_global_device_ids=true, to_apply=%region_34.35.clone | all-reduce | flops 9216 | bytes 73728
  758.5 14.3 %reduce-scatter.31.cloned.1.call-done = bf16[96,192]{1,0:T(8,128)(2,1)} async-done(((bf16[768,192]{1,0:T(8,128)(2,1)}), bf16[96,192]{1,0:T(8,128)(2,1)}) %reduce-scatter.31.cloned.1.call-update) | async-done | bytes 36880 | tf_op jit(solution)/shard_map/reduce_scatter | solution.py:42
  774.2 64.8 %reduce-scatter.29.cloned.1.call-done = bf16[96,576]{1,0:T(8,128)(2,1)} async-done(((bf16[768,576]{1,0:T(8,128)(2,1)}), bf16[96,576]{1,0:T(8,128)(2,1)}) %reduce-scatter.29.cloned.1.call-update) | async-done | bytes 110608 | tf_op jit(solution)/shard_map/reduce_scatter | solution.py:42
  (325 shorter events, 153.0 us)
Async XLA Ops:
  8.0 97.4 %all-gather.31.cloned.1.call-start = ((), (), s32[]{:S(2)}) async-start(), calls=%async_computation.36 | async-start | bytes 1966080 | tf_op jit(solution)/shard_map/all_gather | solution.py:32
  10.6 62.3 %copy-start.45 = (bf16[96,576]{1,0:T(8,128)(2,1)S(1)}, bf16[96,576]{1,0:T(8,128)(2,1)}, u32[]{:S(2)}) copy-start(bf16[96,576]{1,0:T(8,128)(2,1)} %param.20) | copy-start | bytes 331780
  39.0 70.1 %all-gather.29.cloned.1.call-start = ((), (), s32[]{:S(2)}) async-start(), calls=%async_computation.35 | async-start | bytes 1966080 | tf_op jit(solution)/shard_map/all_gather | solution.py:32
  39.7 111.6 %reduce-scatter.13.cloned.1.call-start = ((), (), s32[]{:S(2)}) async-start(), calls=%async_computation.15 | async-start | bytes 1966080 | tf_op jit(solution)/shard_map/reduce_scatter | solution.py:36
  123.7 58.0 %reduce-scatter.17.cloned.1.call-start = ((), (), s32[]{:S(2)}) async-start(), calls=%async_computation.20 | async-start | bytes 1966080 | tf_op jit(solution)/shard_map/reduce_scatter | solution.py:36
  133.9 49.3 %copy-start.25 = (bf16[3,64,1024]{2,1,0:T(8,128)(2,1)}, bf16[3,64,1024]{2,1,0:T(8,128)(2,1)S(1)}, u32[]{:S(2)}) copy-start(bf16[3,64,1024]{2,1,0:T(8,128)(2,1)S(1)} %fusion.46) | copy-start | bytes 1179652
  133.9 50.6 %copy-start.48 = (f32[768]{0:T(1024)S(1)}, f32[768]{0:T(1024)}, u32[]{:S(2)}) copy-start(f32[768]{0:T(1024)} %param.25) | copy-start | bytes 9220
  133.9 50.6 %copy-start.54 = (f32[768]{0:T(1024)S(1)}, f32[768]{0:T(1024)}, u32[]{:S(2)}) copy-start(f32[768]{0:T(1024)} %param.26) | copy-start | bytes 9220
  135.7 53.5 %all-gather.15.cloned.1.call-start = ((), (), s32[]{:S(2)}) async-start(), calls=%async_computation.17 | async-start | bytes 1327104 | tf_op jit(solution)/shard_map/all_gather | solution.py:103
  136.3 70.2 %all-gather.19.cloned.1.call-start = ((), (), s32[]{:S(2)}) async-start(), calls=%async_computation.21 | async-start | bytes 1966080 | tf_op jit(solution)/shard_map/all_gather | solution.py:32
  186.9 41.2 %all-gather.13.cloned.1.call-start = ((), (), s32[]{:S(2)}) async-start(), calls=%async_computation.16 | async-start | bytes 1966080 | tf_op jit(solution)/shard_map/all_gather | solution.py:32
  187.5 84.2 %all-gather.17.cloned.1.call-start = ((), (), s32[]{:S(2)}) async-start(), calls=%async_computation.18 | async-start | bytes 1327104 | tf_op jit(solution)/shard_map/all_gather | solution.py:104
  188.2 115.2 %reduce-scatter.15.cloned.1.call-start = ((), (), s32[]{:S(2)}) async-start(), calls=%async_computation.19 | async-start | bytes 1966080 | tf_op jit(solution)/shard_map/reduce_scatter | solution.py:36
  276.0 57.0 %reduce-scatter.19.cloned.1.call-start = ((), (), s32[]{:S(2)}) async-start(), calls=%async_computation.22 | async-start | bytes 1966080 | tf_op jit(solution)/shard_map/reduce_scatter | solution.py:36
  280.5 52.5 %copy-start.7 = (bf16[256,768]{1,0:T(8,128)(2,1)S(1)}, bf16[256,768]{1,0:T(8,128)(2,1)}, u32[]{:S(2)}) copy-start(bf16[256,768]{1,0:T(8,128)(2,1)} %reduce-scatter.17.cloned.1.call-done) | copy-start | bytes 1179652
  280.5 79.1 %all-gather.21.cloned.1.call-start = ((), (), s32[]{:S(2)}) async-start(), calls=%async_computation.23 | async-start | bytes 1966080 | tf_op jit(solution)/shard_map/all_gather | solution.py:32
  339.9 40.9 %all-gather.25.cloned.1.call-start = ((), (), s32[]{:S(2)}) async-start(), calls=%async_computation.27 | async-start | bytes 1966080 | tf_op jit(solution)/shard_map/all_gather | solution.py:32
  340.8 83.4 %reduce-scatter.21.cloned.1.call-start = ((), (), s32[]{:S(2)}) async-start(), calls=%async_computation.24 | async-start | bytes 1966080 | tf_op jit(solution)/shard_map/reduce_scatter | solution.py:36
  396.1 58.5 %reduce-scatter.25.cloned.1.call-start = ((), (), s32[]{:S(2)}) async-start(), calls=%async_computation.28 | async-start | bytes 1966080 | tf_op jit(solution)/shard_map/reduce_scatter | solution.py:36
  400.5 81.6 %all-gather.27.cloned.1.call-start = ((), (), s32[]{:S(2)}) async-start(), calls=%async_computation.29 | async-start | bytes 1966080 | tf_op jit(solution)/shard_map/all_gather | solution.py:32
  462.4 47.2 %all-gather.23.cloned.1.call-start = ((), (), s32[]{:S(2)}) async-start(), calls=%async_computation.25 | async-start | bytes 1966080 | tf_op jit(solution)/shard_map/all_gather | solution.py:32
  465.8 97.0 %reduce-scatter.27.cloned.1.call-start = ((), (), s32[]{:S(2)}) async-start(), calls=%async_computation.30 | async-start | bytes 1966080 | tf_op jit(solution)/shard_map/reduce_scatter | solution.py:36
  509.3 58.6 %reduce-scatter.23.cloned.1.call-start = ((), (), s32[]{:S(2)}) async-start(), calls=%async_computation.26 | async-start | bytes 1966080 | tf_op jit(solution)/shard_map/reduce_scatter | solution.py:36
  536.9 104.2 %reduce-scatter.35.cloned.1.call-start = ((), (), s32[]{:S(2)}) async-start(), calls=%async_computation.34 | async-start | bytes 1327104 | tf_op jit(solution)/shard_map/reduce_scatter | solution.py:42
  543.1 165.1 %reduce-scatter.33.cloned.1.call-start = ((), (), s32[]{:S(2)}) async-start(), calls=%async_computation.33 | async-start | bytes 1327104 | tf_op jit(solution)/shard_map/reduce_scatter | solution.py:42
  549.7 223.0 %reduce-scatter.31.cloned.1.call-start = ((), (), s32[]{:S(2)}) async-start(), calls=%async_computation.32 | async-start | bytes 442368 | tf_op jit(solution)/shard_map/reduce_scatter | solution.py:42
  557.2 281.9 %reduce-scatter.29.cloned.1.call-start = ((), (), s32[]{:S(2)}) async-start(), calls=%async_computation.31 | async-start | bytes 1105920 | tf_op jit(solution)/shard_map/reduce_scatter | solution.py:42
  568.9 145.5 %copy-start.28 = (bf16[3,64,1024]{2,1,0:T(8,128)(2,1)S(1)}, bf16[3,64,1024]{2,1,0:T(8,128)(2,1)}, u32[]{:S(2)}) copy-start(bf16[3,64,1024]{2,1,0:T(8,128)(2,1)} %copy-done.27) | copy-start | bytes 1179652
  568.9 145.5 %copy-start.30 = (bf16[3,64,1024]{2,1,0:T(8,128)(2,1)S(1)}, bf16[3,64,1024]{2,1,0:T(8,128)(2,1)}, u32[]{:S(2)}) copy-start(bf16[3,64,1024]{2,1,0:T(8,128)(2,1)} %copy-done.29) | copy-start | bytes 1179652
  571.8 268.9 %all-to-all-start.2 = ((bf16[256,2,768]{2,1,0:T(2,128)(2,1)}), bf16[256,2,768]{2,1,0:T(2,128)(2,1)S(1)}, u32[]{:S(2)}, u32[]{:S(2)}) async-start(bf16[256,2,768]{2,1,0:T(2,128)(2,1)} %copy.91), calls=%async_computation.10 | async-start | bytes 1572864 | tf_op jit(solution)/shard_map/all_to_all | solution.py:354
  714.4 127.1 %copy-start.57 = (s32[16]{0:T(128)S(1)}, s32[16]{0:T(128)}, u32[]{:S(2)}) copy-start(s32[16]{0:T(128)} %param.19) | copy-start | bytes 196
  714.4 128.4 %copy-start.1 = (bf16[32,16,768]{2,1,0:T(8,128)(2,1)S(1)}, bf16[32,16,768]{2,1,0:T(8,128)(2,1)}, u32[]{:S(2)}) copy-start(bf16[32,16,768]{2,1,0:T(8,128)(2,1)} %param.17) | copy-start | bytes 2359300
  (65 other events, 601.2 us)
Sparse Core Ops, SparseCore 0:
  39.1 18.6 all-gather.30
  59.9 19.6 all-gather.28
  123.8 27.3 reduce-scatter.12
  153.7 27.9 reduce-scatter.16
  340.0 19.6 all-gather.20
  361.1 19.6 all-gather.24
  462.5 19.6 all-gather.26
  483.7 19.6 all-gather.22
  509.4 27.9 reduce-scatter.26
  539.8 27.9 reduce-scatter.22
  571.2 69.7 reduce-scatter.34
  644.3 63.8 reduce-scatter.32
  711.5 61.2 reduce-scatter.30
  776.0 63.0 reduce-scatter.28
Sparse Core Ops, SparseCore 1:
  138.4 40.5 all-gather.14
  187.0 19.5 all-gather.18
  208.5 19.5 all-gather.12
  230.3 41.4 all-gather.16
  276.1 26.3 reduce-scatter.14
  305.0 27.9 reduce-scatter.18
  396.2 27.9 reduce-scatter.20
  426.6 27.9 reduce-scatter.24
where the time goes:
time: 859 us; the launch traced here: 850 us
  waiting for transfers between devices  452 us (53%)
  blocking collectives  153 us (18%)
  matrix products  136 us (16%)
  other arithmetic  55.4 us (6%)
  local copies, waits for them, and re-layouts  28.8 us (3%)
  between operations  16.9 us (2%)
    reduce_scatter x4, waiting for transfers between devices, scatter_weight(): lax.psum_scatter(grad.astype(jnp.bfloat16), 'dp', scatter_dimension=0, ti...  208 us
    reduce_scatter x8, waiting for transfers between devices, scatter_rows(): lax.psum_scatter(partial_sum.astype(jnp.bfloat16), 'tensor', scatter_dime...  131 us
    all_gather x8, waiting for transfers between devices, gather_rows(): return lax.all_gather(block, 'tensor', axis=0, tiled=True)  84.8 us
    unnamed x1, blocking collectives  40.2 us
    all_gather x1, blocking collectives, on_device(): project_full = lax.all_gather(project_weight, 'dp', axis=0, tiled=True)  32.5 us
    all_gather x1, blocking collectives, on_device(): lax.all_gather(attention_output_weight, 'dp', axis=0, tiled=True)  31.2 us
    all_to_all x1, blocking collectives, on_device(): lax.all_to_all(send_tokens, 'dp', split_axis=1, concat_axis=0, tiled=True)  27.4 us
    all_gather x1, waiting for transfers between devices, on_device(): down_full = lax.all_gather(feed_output_weight, 'dp', axis=0, tiled=True)  26.3 us
  transfers between devices with their start and end apart: 23, of which 16 were waited for; matrix products, arithmetic and copies ran while one was open for 18% of the time, Pallas kernels for 0%

commit v1 on v0

--- a/solution.py
+++ b/solution.py
@@ -9,6 +9,24 @@
 MASKED = -1e30
 
 
+def ring_gather(array, axis, dim):
+    ways, here, step = (lax.axis_size(axis), lax.axis_index(axis), array.shape[dim])
+    lengths = [n * ways if d == dim else n for d, n in enumerate(array.shape)]
+    full = lax.dynamic_update_slice_in_dim(
+        jnp.zeros(lengths, array.dtype), array, here * step, axis=dim
+    )
+    going_up = going_down = array
+    for far in range(1, ways // 2 + 1):
+        going_up = lax.ppermute(going_up, axis, [(d, (d + 1) % ways) for d in range(ways)])
+        full = lax.dynamic_update_slice_in_dim(full, going_up, (here - far) % ways * step, axis=dim)
+        if 2 * far < ways:
+            going_down = lax.ppermute(going_down, axis, [(d, (d - 1) % ways) for d in range(ways)])
+            full = lax.dynamic_update_slice_in_dim(
+                full, going_down, (here + far) % ways * step, axis=dim
+            )
+    return full
+
+
 def norm_forward(value, gain, shift):
     centred = value - jnp.mean(value, axis=-1, keepdims=True)
     inverse = lax.rsqrt(jnp.mean(centred * centred, axis=-1, keepdims=True) + EPSILON)
@@ -29,7 +47,7 @@
 
 
 def gather_rows(block):
-    return lax.all_gather(block, "tensor", axis=0, tiled=True)
+    return ring_gather(block, "tensor", 0)
 
 
 def scatter_rows(partial_sum):

time: 859 us -> 823 us (0.958)
  waiting for transfers between devices: 452 us -> 422 us
  starting transfers between devices: 8.07 us -> 25.1 us
  matrix products: 136 us -> 120 us
  local copies, waits for them, and re-layouts: 28.8 us -> 44 us
  blocking collectives: 153 us -> 140 us
  other arithmetic: 55.4 us -> 45.9 us
    all_gather x8 -> x0, waiting for transfers between devices: 84.8 us -> none  [gather_rows(): return lax.all_gather(block, 'tensor', axis=0, tiled=True)]
    ppermute x0 -> x24, waiting for transfers between devices: none -> 80.8 us  [the longest x16 72.6 us: ring_gather(): lax.ppermute(going_up, axis, [(d, (d + 1) % ways) for d in range(ways)])]
    all_to_all x1 -> x0, blocking collectives: 27.4 us -> none  [on_device(): lax.all_to_all(send_tokens, 'dp', split_axis=1, concat_axis=0, tiled=True)]
    all_gather x1, waiting for transfers between devices: 26.3 us -> 0.01 us  [on_device(): down_full = lax.all_gather(feed_output_weight, 'dp', axis=0, tiled=True)]
    ppermute x0 -> x24, starting transfers between devices: none -> 10.7 us  [the longest x8 8.91 us: ring_gather(): lax.ppermute(going_down, axis, [(d, (d - 1) % ways) for d in range(ways)])]
    all_gather x1, blocking collectives: 31.2 us -> 40.7 us  [on_device(): lax.all_gather(attention_output_weight, 'dp', axis=0, tiled=True)]
    dynamic_update_slice x0 -> x26, local copies, waits for them, and re-layouts: none -> 9.35 us  [the longest x16 6.31 us: ring_gather(): lax.dynamic_update_slice_in_dim(full, going_up, (here - far) % ways * ste...]
    dot_general x2, matrix products: 16.3 us -> 7.32 us  [on_device(): jnp.dot(grad_feed_full[s], down_full, preferred_element_type=jnp.float32)]
  transfers between devices with their start and end apart: 23 -> 40, of which waited for: 16 -> 26; matrix products, arithmetic and copies ran while one was open for 18% -> 19% of each run, Pallas kernels for 0% -> 0%
where the time goes in v1:
time: 823 us; the launch traced here: 815 us
  waiting for transfers between devices  422 us (51%)
  blocking collectives  140 us (17%)
  matrix products  120 us (15%)
  other arithmetic  45.9 us (6%)
  local copies, waits for them, and re-layouts  44 us (5%)
  starting transfers between devices  25.1 us (3%)
  between operations  17.9 us (2%)
    reduce_scatter x4, waiting for transfers between devices, scatter_weight(): lax.psum_scatter(grad.astype(jnp.bfloat16), 'dp', scatter_dimension=0, ti...  212 us
    reduce_scatter x8, waiting for transfers between devices, scatter_rows(): lax.psum_scatter(partial_sum.astype(jnp.bfloat16), 'tensor', scatter_dime...  128 us
    ppermute x16, waiting for transfers between devices, ring_gather(): lax.ppermute(going_up, axis, [(d, (d + 1) % ways) for d in range(ways)])  72.6 us
    all_gather x1, blocking collectives, on_device(): lax.all_gather(attention_output_weight, 'dp', axis=0, tiled=True)  40.7 us
    unnamed x1, blocking collectives  40.2 us
    all_gather x1, blocking collectives, on_device(): project_full = lax.all_gather(project_weight, 'dp', axis=0, tiled=True)  34.9 us
    all_to_all x1, blocking collectives, on_device(): lax.all_to_all(send_grad, 'dp', split_axis=1, concat_axis=0, tiled=True)  23.7 us
    unnamed x224, local copies, waits for them, and re-layouts  22.7 us
  transfers between devices with their start and end apart: 40, of which 26 were waited for; matrix products, arithmetic and copies ran while one was open for 19% of the time, Pallas kernels for 0%

profile of v1, /device:TPU:0, one launch (start us, length us, event | category | flops | bytes accessed | tf_op | source)
XLA Modules:
  0.0 814.5 jit_solution(14738290767401045499)
XLA Ops:
  11.4 7.3 all-to-all-start
  20.8 40.7 %all_gather.13 = bf16[768,192]{1,0:T(8,128)(2,1)S(1)} all-gather(bf16[96,192]{1,0:T(8,128)(2,1)S(1)} %copy-done.67), channel_id=1, replica_groups=mesh['dp'=8,'tensor'=4] {'dp'}, dimensions={0}, use_global_device_ids=true | all-gather | bytes 331776 | tf_op jit(solution)/shard_map/all_gather | solution.py:120
  61.5 34.9 %all_gather.12 = bf16[768,576]{1,0:T(8,128)(2,1)} all-gather(bf16[96,576]{1,0:T(8,128)(2,1)S(1)} %copy-done.60), channel_id=1, replica_groups=mesh['dp'=8,'tensor'=4] {'dp'}, dimensions={0}, use_global_device_ids=true | all-gather | bytes 995328 | tf_op jit(solution)/shard_map/all_gather | solution.py:119
  100.4 5.9 collective-permute-done
  106.2 8.4 %collective-permute-done.6 = bf16[256,768]{1,0:T(8,128)(2,1)S(1)} collective-permute-done((bf16[256,768]{1,0:T(8,128)(2,1)S(1)}, bf16[256,768]{1,0:T(8,128)(2,1)S(1)}, u32[]{:S(2)}, u32[]{:S(2)}) %collective-permute-start.6) | collective-permute-done | bytes 393248 | tf_op jit(solution)/shard_map/ppermute | solution.py:20
  150.2 9.1 %reduce-scatter.13.cloned.1.call-done = bf16[256,768]{1,0:T(8,128)(2,1)} async-done(((bf16[1024,768]{1,0:T(8,128)(2,1)}), bf16[256,768]{1,0:T(8,128)(2,1)}) %reduce-scatter.13.cloned.1.call-update) | async-done | bytes 393232 | tf_op jit(solution)/shard_map/reduce_scatter | solution.py:54
  160.6 29.3 %reduce-scatter.17.cloned.1.call-done = bf16[256,768]{1,0:T(8,128)(2,1)} async-done(((bf16[1024,768]{1,0:T(8,128)(2,1)}), bf16[256,768]{1,0:T(8,128)(2,1)}) %reduce-scatter.17.cloned.1.call-update) | async-done | bytes 393232 | tf_op jit(solution)/shard_map/reduce_scatter | solution.py:54
  202.7 7.4 collective-permute-done.9
  227.6 17.3 %multiply_convert_fusion.3 = (bf16[1024,768]{1,0:T(8,128)(2,1)}, f32[1024,768]{1,0:T(8,128)}, bf16[1024,768]{1,0:T(8,128)(2,1)}, f32[1024,768]{1,0:T(8,128)}, f32[1024,768]{1,0:T(8,128)}) fusion(f32[768]{0:T(1024)S(1)} %dynamic_slice.11, f32[1024,768]{1,0:T(8,128)S(1)} %fusion.110, bf16[1024,768]{1,0:T(8,128)(2,1)S(1)} %constant_dynamic-update-slice_fusion.24, ...), kind=kOutput, calls=%fused_computation.43 | convolution fusion | flops 1311768576 | bytes 18484224 | tf_op jit(solution)/shard_map/dot_general | solution.py:225
  249.4 4.4 convolution_convert_fusion.4
  254.6 23.7 %all_to_all.54 = bf16[32,16,768]{2,0,1:T(8,128)(2,1)S(1)} all-to-all(bf16[32,16,768]{2,0,1:T(8,128)(2,1)S(1)} %copy.83), channel_id=1, replica_groups=mesh['dp'=8,'tensor'=4] {'dp'}, dimensions={1} | all-to-all | bytes 1572864 | tf_op jit(solution)/shard_map/all_to_all | solution.py:108
  278.4 29.6 %reduce-scatter.19.cloned.1.call-done = bf16[256,768]{1,0:T(8,128)(2,1)} async-done(((bf16[1024,768]{1,0:T(8,128)(2,1)}), bf16[256,768]{1,0:T(8,128)(2,1)}) %reduce-scatter.19.cloned.1.call-update) | async-done | bytes 393232 | tf_op jit(solution)/shard_map/reduce_scatter | solution.py:54
  317.9 5.9 collective-permute-done.18
  323.8 8.4 %collective-permute-done.12 = bf16[256,768]{1,0:T(8,128)(2,1)S(1)} collective-permute-done((bf16[256,768]{1,0:T(8,128)(2,1)S(1)}, bf16[256,768]{1,0:T(8,128)(2,1)S(1)}, u32[]{:S(2)}, u32[]{:S(2)}) %collective-permute-start.12) | collective-permute-done | bytes 393248 | tf_op jit(solution)/shard_map/ppermute | solution.py:20
  335.4 7.2 collective-permute-done.14
  347.6 5.9 convert_reduce_fusion
  361.8 23.7 %reduce-scatter.25.cloned.1.call-done = bf16[256,768]{1,0:T(8,128)(2,1)} async-done(((bf16[1024,768]{1,0:T(8,128)(2,1)}), bf16[256,768]{1,0:T(8,128)(2,1)}) %reduce-scatter.25.cloned.1.call-update) | async-done | bytes 393232 | tf_op jit(solution)/shard_map/reduce_scatter | solution.py:54
  385.5 30.4 %reduce-scatter.21.cloned.1.call-done = bf16[256,768]{1,0:T(8,128)(2,1)} async-done(((bf16[1024,768]{1,0:T(8,128)(2,1)}), bf16[256,768]{1,0:T(8,128)(2,1)}) %reduce-scatter.21.cloned.1.call-update) | async-done | bytes 393232 | tf_op jit(solution)/shard_map/reduce_scatter | solution.py:54
  424.2 6.8 collective-permute-done.15
  431.1 8.5 %collective-permute-done.21 = bf16[256,768]{1,0:T(8,128)(2,1)} collective-permute-done((bf16[256,768]{1,0:T(8,128)(2,1)S(1)}, bf16[256,768]{1,0:T(8,128)(2,1)}, u32[]{:S(2)}, u32[]{:S(2)}) %collective-permute-start.21) | collective-permute-done | bytes 393248 | tf_op jit(solution)/shard_map/ppermute | solution.py:20
  446.6 6.1 multiply_reduce_fusion.1
  456.5 5.2 multiply_convert_fusion.1
  473.3 6.1 multiply_reduce_fusion
  482.3 5.3 multiply_convert_fusion
  487.5 4.4 fusion.29
  526.3 5.5 reduce-scatter.27.cloned.1.call-done
  535.8 5.7 all-to-all-start.2
  542.3 63.0 %reduce-scatter.35.cloned.1.call-done = bf16[96,768]{1,0:T(8,128)(2,1)} async-done(((bf16[768,768]{1,0:T(8,128)(2,1)}), bf16[96,768]{1,0:T(8,128)(2,1)}) %reduce-scatter.35.cloned.1.call-update) | async-done | bytes 147472 | tf_op jit(solution)/shard_map/reduce_scatter | solution.py:60
  606.9 65.4 %reduce-scatter.33.cloned.1.call-done = bf16[96,768]{1,0:T(8,128)(2,1)} async-done(((bf16[768,768]{1,0:T(8,128)(2,1)}), bf16[96,768]{1,0:T(8,128)(2,1)}) %reduce-scatter.33.cloned.1.call-update) | async-done | bytes 147472 | tf_op jit(solution)/shard_map/reduce_scatter | solution.py:60
  675.6 40.2 %all-reduce.2 = (f32[32,48]{1,0:T(8,128)S(1)}, f32[32,240]{1,0:T(8,128)S(1)}) all-reduce(f32[32,48]{1,0:T(8,128)S(1)} %pad_maximum_fusion.4, f32[32,240]{1,0:T(8,128)S(1)} %concatenate.21), channel_id=11, replica_groups=mesh['dp'=8,'tensor'=4] {'dp','tensor'}, use_global_device_ids=true, to_apply=%region_34.35.clone | all-reduce | flops 9216 | bytes 73728
  717.5 19.2 %reduce-scatter.31.cloned.1.call-done = bf16[96,192]{1,0:T(8,128)(2,1)} async-done(((bf16[768,192]{1,0:T(8,128)(2,1)}), bf16[96,192]{1,0:T(8,128)(2,1)}) %reduce-scatter.31.cloned.1.call-update) | async-done | bytes 36880 | tf_op jit(solution)/shard_map/reduce_scatter | solution.py:60
  738.2 64.9 %reduce-scatter.29.cloned.1.call-done = bf16[96,576]{1,0:T(8,128)(2,1)} async-done(((bf16[768,576]{1,0:T(8,128)(2,1)}), bf16[96,576]{1,0:T(8,128)(2,1)}) %reduce-scatter.29.cloned.1.call-update) | async-done | bytes 110608 | tf_op jit(solution)/shard_map/reduce_scatter | solution.py:60
  (460 shorter events, 190.8 us)
Async XLA Ops:
  11.4 85.0 %all-to-all-start = ((bf16[32,16,768]{2,0,1:T(8,128)(2,1)}), bf16[32,16,768]{2,0,1:T(8,128)(2,1)S(1)}, u32[]{:S(2)}, u32[]{:S(2)}) async-start(bf16[32,16,768]{2,0,1:T(8,128)(2,1)} %copy.78), calls=%async_computation | async-start | bytes 1572864 | tf_op jit(solution)/shard_map/all_to_all | solution.py:107
  18.7 140.6 %reduce-scatter.13.cloned.1.call-start = ((), (), s32[]{:S(2)}) async-start(), calls=%async_computation.15 | async-start | bytes 1966080 | tf_op jit(solution)/shard_map/reduce_scatter | solution.py:54
  96.6 18.2 %collective-permute-start.1 = (bf16[256,768]{1,0:T(8,128)(2,1)S(1)}, bf16[256,768]{1,0:T(8,128)(2,1)S(1)}, u32[]{:S(2)}, u32[]{:S(2)}) collective-permute-start(bf16[256,768]{1,0:T(8,128)(2,1)S(1)} %get-tuple-element.147), channel_id=1, source_target_pairs={{0,3},{1,0},{2,1},{3,2},{4,7},{5,4},{6,5},{7,6},{8,11},{9,8},{10,9... | collective-permute-start | bytes 1179656 | tf_op jit(solution)/shard_map/ppermute | solution.py:23
  98.3 16.4 %collective-permute-start.6 = (bf16[256,768]{1,0:T(8,128)(2,1)S(1)}, bf16[256,768]{1,0:T(8,128)(2,1)S(1)}, u32[]{:S(2)}, u32[]{:S(2)}) collective-permute-start(bf16[256,768]{1,0:T(8,128)(2,1)S(1)} %get-tuple-element.148), channel_id=1, source_target_pairs={{0,1},{1,2},{2,3},{3,0},{4,5},{5,6},{6,7},{7,4},{8,9},{9,10},{10,1... | collective-permute-start | bytes 1179656 | tf_op jit(solution)/shard_map/ppermute | solution.py:20
  98.3 17.9 %collective-permute-start.7 = (bf16[256,768]{1,0:T(8,128)(2,1)S(1)}, bf16[256,768]{1,0:T(8,128)(2,1)S(1)}, u32[]{:S(2)}, u32[]{:S(2)}) collective-permute-start(bf16[256,768]{1,0:T(8,128)(2,1)S(1)} %get-tuple-element.148), channel_id=1, source_target_pairs={{0,3},{1,0},{2,1},{3,2},{4,7},{5,4},{6,5},{7,6},{8,11},{9,8},{10,9... | collective-permute-start | bytes 1179656 | tf_op jit(solution)/shard_map/ppermute | solution.py:23
  106.2 14.4 %collective-permute-start.2 = (bf16[256,768]{1,0:T(8,128)(2,1)S(1)}, bf16[256,768]{1,0:T(8,128)(2,1)S(1)}, u32[]{:S(2)}, u32[]{:S(2)}) collective-permute-start(bf16[256,768]{1,0:T(8,128)(2,1)S(1)} %collective-permute-done), channel_id=1, source_target_pairs={{0,1},{1,2},{2,3},{3,0},{4,5},{5,6},{6,7},{7,4},{8,9},{9,10},{10,1... | collective-permute-start | bytes 1179656 | tf_op jit(solution)/shard_map/ppermute | solution.py:20
  114.7 19.8 %collective-permute-start.8 = (bf16[256,768]{1,0:T(8,128)(2,1)S(1)}, bf16[256,768]{1,0:T(8,128)(2,1)S(1)}, u32[]{:S(2)}, u32[]{:S(2)}) collective-permute-start(bf16[256,768]{1,0:T(8,128)(2,1)S(1)} %collective-permute-done.6), channel_id=1, source_target_pairs={{0,1},{1,2},{2,3},{3,0},{4,5},{5,6},{6,7},{7,4},{8,9},{9,10},{10,1... | collective-permute-start | bytes 1179656 | tf_op jit(solution)/shard_map/ppermute | solution.py:20
  134.0 56.0 %reduce-scatter.17.cloned.1.call-start = ((), (), s32[]{:S(2)}) async-start(), calls=%async_computation.19 | async-start | bytes 1966080 | tf_op jit(solution)/shard_map/reduce_scatter | solution.py:54
  149.6 73.0 %all-gather.3.cloned.1.call-start = ((), (), s32[]{:S(2)}) async-start(), calls=%async_computation.16 | async-start | bytes 1327104 | tf_op jit(solution)/shard_map/all_gather | solution.py:121
  150.2 94.8 %all-gather.5.cloned.1.call-start = ((), (), s32[]{:S(2)}) async-start(), calls=%async_computation.17 | async-start | bytes 1327104 | tf_op jit(solution)/shard_map/all_gather | solution.py:122
  196.5 15.5 %collective-permute-start.4 = (bf16[256,768]{1,0:T(8,128)(2,1)}, bf16[256,768]{1,0:T(8,128)(2,1)}, u32[]{:S(2)}, u32[]{:S(2)}) collective-permute-start(bf16[256,768]{1,0:T(8,128)(2,1)} %get-tuple-element.128), channel_id=1, source_target_pairs={{0,3},{1,0},{2,1},{3,2},{4,7},{5,4},{6,5},{7,6},{8,11},{9,8},{10,9... | collective-permute-start | bytes 1179656 | tf_op jit(solution)/shard_map/ppermute | solution.py:23
  197.8 18.2 %collective-permute-start.10 = (bf16[256,768]{1,0:T(8,128)(2,1)}, bf16[256,768]{1,0:T(8,128)(2,1)}, u32[]{:S(2)}, u32[]{:S(2)}) collective-permute-start(bf16[256,768]{1,0:T(8,128)(2,1)} %get-tuple-element.134), channel_id=1, source_target_pairs={{0,3},{1,0},{2,1},{3,2},{4,7},{5,4},{6,5},{7,6},{8,11},{9,8},{10,9... | collective-permute-start | bytes 1179656 | tf_op jit(solution)/shard_map/ppermute | solution.py:23
  198.3 80.1 %reduce-scatter.15.cloned.1.call-start = ((), (), s32[]{:S(2)}) async-start(), calls=%async_computation.18 | async-start | bytes 1966080 | tf_op jit(solution)/shard_map/reduce_scatter | solution.py:54
  201.7 16.2 %collective-permute-start.5 = (bf16[256,768]{1,0:T(8,128)(2,1)}, bf16[256,768]{1,0:T(8,128)(2,1)S(1)}, u32[]{:S(2)}, u32[]{:S(2)}) collective-permute-start(bf16[256,768]{1,0:T(8,128)(2,1)} %collective-permute-done.3), channel_id=1, source_target_pairs={{0,1},{1,2},{2,3},{3,0},{4,5},{5,6},{6,7},{7,4},{8,9},{9,10},{10,1... | collective-permute-start | bytes 1179656 | tf_op jit(solution)/shard_map/ppermute | solution.py:20
  249.3 58.7 %reduce-scatter.19.cloned.1.call-start = ((), (), s32[]{:S(2)}) async-start(), calls=%async_computation.20 | async-start | bytes 1966080 | tf_op jit(solution)/shard_map/reduce_scatter | solution.py:54
  253.8 131.7 %reduce-scatter.25.cloned.1.call-start = ((), (), s32[]{:S(2)}) async-start(), calls=%async_computation.23 | async-start | bytes 1966080 | tf_op jit(solution)/shard_map/reduce_scatter | solution.py:54
  315.7 16.5 %collective-permute-start.12 = (bf16[256,768]{1,0:T(8,128)(2,1)S(1)}, bf16[256,768]{1,0:T(8,128)(2,1)S(1)}, u32[]{:S(2)}, u32[]{:S(2)}) collective-permute-start(bf16[256,768]{1,0:T(8,128)(2,1)S(1)} %get-tuple-element.121), channel_id=1, source_target_pairs={{0,1},{1,2},{2,3},{3,0},{4,5},{5,6},{6,7},{7,4},{8,9},{9,10},{10,1... | collective-permute-start | bytes 1179656 | tf_op jit(solution)/shard_map/ppermute | solution.py:20
  316.1 16.4 %collective-permute-start.19 = (bf16[256,768]{1,0:T(8,128)(2,1)S(1)}, bf16[256,768]{1,0:T(8,128)(2,1)S(1)}, u32[]{:S(2)}, u32[]{:S(2)}) collective-permute-start(bf16[256,768]{1,0:T(8,128)(2,1)S(1)} %get-tuple-element.119), channel_id=1, source_target_pairs={{0,3},{1,0},{2,1},{3,2},{4,7},{5,4},{6,5},{7,6},{8,11},{9,8},{10,9... | collective-permute-start | bytes 1179656 | tf_op jit(solution)/shard_map/ppermute | solution.py:23
  317.4 17.9 %collective-permute-start.13 = (bf16[256,768]{1,0:T(8,128)(2,1)S(1)}, bf16[256,768]{1,0:T(8,128)(2,1)S(1)}, u32[]{:S(2)}, u32[]{:S(2)}) collective-permute-start(bf16[256,768]{1,0:T(8,128)(2,1)S(1)} %get-tuple-element.121), channel_id=1, source_target_pairs={{0,3},{1,0},{2,1},{3,2},{4,7},{5,4},{6,5},{7,6},{8,11},{9,8},{10,9... | collective-permute-start | bytes 1179656 | tf_op jit(solution)/shard_map/ppermute | solution.py:23
  323.8 20.4 %collective-permute-start.20 = (bf16[256,768]{1,0:T(8,128)(2,1)S(1)}, bf16[256,768]{1,0:T(8,128)(2,1)S(1)}, u32[]{:S(2)}, u32[]{:S(2)}) collective-permute-start(bf16[256,768]{1,0:T(8,128)(2,1)S(1)} %collective-permute-done.18), channel_id=1, source_target_pairs={{0,1},{1,2},{2,3},{3,0},{4,5},{5,6},{6,7},{7,4},{8,9},{9,10},{10,1... | collective-permute-start | bytes 1179656 | tf_op jit(solution)/shard_map/ppermute | solution.py:20
  357.3 58.6 %reduce-scatter.21.cloned.1.call-start = ((), (), s32[]{:S(2)}) async-start(), calls=%async_computation.21 | async-start | bytes 1966080 | tf_op jit(solution)/shard_map/reduce_scatter | solution.py:54
  361.7 162.7 %reduce-scatter.23.cloned.1.call-start = ((), (), s32[]{:S(2)}) async-start(), calls=%async_computation.22 | async-start | bytes 1966080 | tf_op jit(solution)/shard_map/reduce_scatter | solution.py:54
  422.3 17.3 %collective-permute-start.21 = (bf16[256,768]{1,0:T(8,128)(2,1)S(1)}, bf16[256,768]{1,0:T(8,128)(2,1)}, u32[]{:S(2)}, u32[]{:S(2)}) collective-permute-start(bf16[256,768]{1,0:T(8,128)(2,1)S(1)} %get-tuple-element.117), channel_id=1, source_target_pairs={{0,1},{1,2},{2,3},{3,0},{4,5},{5,6},{6,7},{7,4},{8,9},{9,10},{10,1... | collective-permute-start | bytes 1179656 | tf_op jit(solution)/shard_map/ppermute | solution.py:20
  422.4 18.8 %collective-permute-start.16 = (bf16[256,768]{1,0:T(8,128)(2,1)S(1)}, bf16[256,768]{1,0:T(8,128)(2,1)S(1)}, u32[]{:S(2)}, u32[]{:S(2)}) collective-permute-start(bf16[256,768]{1,0:T(8,128)(2,1)S(1)} %get-tuple-element.115), channel_id=1, source_target_pairs={{0,3},{1,0},{2,1},{3,2},{4,7},{5,4},{6,5},{7,6},{8,11},{9,8},{10,9... | collective-permute-start | bytes 1179656 | tf_op jit(solution)/shard_map/ppermute | solution.py:23
  424.2 17.9 %collective-permute-start.22 = (bf16[256,768]{1,0:T(8,128)(2,1)S(1)}, bf16[256,768]{1,0:T(8,128)(2,1)S(1)}, u32[]{:S(2)}, u32[]{:S(2)}) collective-permute-start(bf16[256,768]{1,0:T(8,128)(2,1)S(1)} %get-tuple-element.117), channel_id=1, source_target_pairs={{0,3},{1,0},{2,1},{3,2},{4,7},{5,4},{6,5},{7,6},{8,11},{9,8},{10,9... | collective-permute-start | bytes 1179656 | tf_op jit(solution)/shard_map/ppermute | solution.py:23
  439.6 28.8 %collective-permute-start.23 = (bf16[256,768]{1,0:T(8,128)(2,1)}, bf16[256,768]{1,0:T(8,128)(2,1)}, u32[]{:S(2)}, u32[]{:S(2)}) collective-permute-start(bf16[256,768]{1,0:T(8,128)(2,1)} %collective-permute-done.21), channel_id=1, source_target_pairs={{0,1},{1,2},{2,3},{3,0},{4,5},{5,6},{6,7},{7,4},{8,9},{9,10},{10,1... | collective-permute-start | bytes 1179656 | tf_op jit(solution)/shard_map/ppermute | solution.py:20
  473.1 58.8 %reduce-scatter.27.cloned.1.call-start = ((), (), s32[]{:S(2)}) async-start(), calls=%async_computation.24 | async-start | bytes 1966080 | tf_op jit(solution)/shard_map/reduce_scatter | solution.py:54
  499.2 106.0 %reduce-scatter.35.cloned.1.call-start = ((), (), s32[]{:S(2)}) async-start(), calls=%async_computation.28 | async-start | bytes 1327104 | tf_op jit(solution)/shard_map/reduce_scatter | solution.py:60
  505.4 166.9 %reduce-scatter.33.cloned.1.call-start = ((), (), s32[]{:S(2)}) async-start(), calls=%async_computation.27 | async-start | bytes 1327104 | tf_op jit(solution)/shard_map/reduce_scatter | solution.py:60
  511.8 225.0 %reduce-scatter.31.cloned.1.call-start = ((), (), s32[]{:S(2)}) async-start(), calls=%async_computation.26 | async-start | bytes 442368 | tf_op jit(solution)/shard_map/reduce_scatter | solution.py:60
  518.8 284.3 %reduce-scatter.29.cloned.1.call-start = ((), (), s32[]{:S(2)}) async-start(), calls=%async_computation.25 | async-start | bytes 1105920 | tf_op jit(solution)/shard_map/reduce_scatter | solution.py:60
  535.8 268.9 %all-to-all-start.2 = ((bf16[256,2,768]{2,1,0:T(2,128)(2,1)}), bf16[256,2,768]{2,1,0:T(2,128)(2,1)S(1)}, u32[]{:S(2)}, u32[]{:S(2)}) async-start(bf16[256,2,768]{2,1,0:T(2,128)(2,1)} %copy.91), calls=%async_computation.10 | async-start | bytes 1572864 | tf_op jit(solution)/shard_map/all_to_all | solution.py:372
  (119 other events, 2423.9 us)
Sparse Core Ops, SparseCore 0:
  134.1 25.1 reduce-scatter.12
  161.8 28.0 reduce-scatter.16
  249.4 28.0 reduce-scatter.14
  279.9 28.0 reduce-scatter.18
  357.4 27.9 reduce-scatter.24
  387.9 27.9 reduce-scatter.20
  473.2 28.0 reduce-scatter.22
  503.8 27.9 reduce-scatter.26
  535.2 69.9 reduce-scatter.34
  608.5 63.7 reduce-scatter.32
  675.6 61.1 reduce-scatter.30
  740.0 63.0 reduce-scatter.28
Sparse Core Ops, SparseCore 1:
  152.3 38.6 all-gather.2
  198.4 41.3 all-gather.4
